TPU v7x, 256 devices: a whole 4x4x8 slice. The times are simulated.
256 devices in a mesh: tr: 4 (over x), tc: 4 (over y_hi, core), st: 16 (over y_lo, z).
Axes of the slice: x: 4, y: 4 (y_hi: 2, y_lo: 2; y = y_hi * 2 + y_lo), z: 8, core: 2. Of those that a mesh axis runs over, the one named last changes fastest.
Arguments:
- teacher_hidden: bfloat16 [256, 28672], P(None, 'st'), may hold values from -6 to 6
- teacher_residual: bfloat16 [256, 8192], P(None, ('tr', 'tc')), may hold values from -6 to 6
- teacher_down: bfloat16 [28672, 8192], P('st', ('tr', 'tc')), may hold values from -0.03125 to 0.03125
- student_input: bfloat16 [256, 4096], P(None, 'st'), may hold values from -6 to 6
- student_stream: bfloat16 [256, 4096], P(None, 'st'), may hold values from -6 to 6
- student_gate: bfloat16 [4096, 14336], P('st', ('tr', 'tc')), may hold values from -0.09375 to 0.09375
- student_up: bfloat16 [4096, 14336], P('st', ('tr', 'tc')), may hold values from -0.09375 to 0.09375
- student_down: bfloat16 [14336, 4096], P(('tr', 'tc'), 'st'), may hold values from -0.046875 to 0.046875
- head: bfloat16 [4096, 8192], P('st', ('tr', 'tc')), may hold values from -0.09375 to 0.09375
Outputs:
- grad_gate: float32 [4096, 14336], P('st', ('tr', 'tc'))
- grad_up: float32 [4096, 14336], P('st', ('tr', 'tc'))
- grad_down: float32 [14336, 4096], P(('tr', 'tc'), 'st')
- grad_head: float32 [4096, 8192], P('st', ('tr', 'tc'))
All inputs are finite; a program needn't handle non-finite values.
Results may differ from a plain program's by a relative error of at most 0.0065.
Values may be sent and summed in bfloat16 or wider, within the bound.
A program may use at most 64 MiB of HBM per device.

v0:
```python
import math

import jax
import jax.numpy as jnp
from jax import lax
from jax.sharding import PartitionSpec as P


def split_up(array, dim, length):
    before, after = (array.shape[:dim], array.shape[dim + 1 :])
    return jnp.moveaxis(array.reshape(*before, length, -1, *after), dim, 0)


def sent_and_summed(array, axis, dim):
    length = lax.axis_size(axis)
    pieces = lax.all_to_all(split_up(array, dim, length), axis, 0, 0, tiled=True)
    return jnp.sum(pieces, axis=0)


def side_by_side(arrays, axis, dim, along):
    ends, at = ([], 0)
    for a in arrays[:-1]:
        at += a.shape[along]
        ends.append(at)
    both = jnp.concatenate(arrays, axis=along)
    return tuple(jnp.split(sent_and_summed(both, axis, dim), ends, axis=along))


def laid_out(pieces, dim):
    shape = list(pieces.shape[1:])
    shape[dim] *= pieces.shape[0]
    return jnp.moveaxis(pieces, 0, dim).reshape(shape)


def copy_for_each(array, axis):
    length = lax.axis_size(axis)
    return lax.all_to_all(
        jnp.broadcast_to(array[None], (length, *array.shape)), axis, 0, 0, tiled=True
    )


def gathered_copies(array, axis, dim):
    return laid_out(copy_for_each(array, axis), dim)


def filled_up(lines, length):
    spare = -len(lines) % length
    return jnp.pad(lines, [(0, spare)] + [(0, 0)] * (lines.ndim - 1))


def sum_by_parts(array, axes):
    lines = array.reshape(-1, array.shape[-1])
    padded = filled_up(lines, lax.axis_size(axes))
    whole = gathered_copies(sent_and_summed(padded, axes, 0), axes, 0)
    return lax.slice_in_dim(whole, 0, len(lines)).reshape(array.shape)


def sent_together(arrays, axis, dim, along):
    ends, at = ([], 0)
    for a in arrays[:-1]:
        at += a.shape[along]
        ends.append(at)
    both = jnp.concatenate(arrays, axis=along)
    return tuple(jnp.split(lax.all_gather(both, axis, axis=dim, tiled=True), ends, axis=along))


def contract_rows(left, right):
    return lax.dot_general(
        left, right, (((0,), (0,)), ((), ())), preferred_element_type=jnp.float32
    )


def contract_cols(left, right):
    return lax.dot_general(
        left, right, (((1,), (1,)), ((), ())), preferred_element_type=jnp.float32
    )


def activation_grads(hidden_grad, gate, up):
    sigma = jax.nn.sigmoid(gate)
    gated = gate * sigma
    slope = sigma * (1.0 + gate * (1.0 - sigma))
    return (
        (hidden_grad * up * slope).astype(jnp.bfloat16),
        (hidden_grad * gated).astype(jnp.bfloat16),
    )


def body(
    teacher_hidden,
    teacher_residual,
    teacher_down,
    student_input,
    student_stream,
    student_gate,
    student_up,
    student_down,
    head,
):
    tokens = student_input.shape[0]
    loss_scale = 1.0 / math.sqrt(tokens)
    teacher_term = jnp.dot(teacher_hidden, teacher_down, preferred_element_type=jnp.float32)
    gate_part = jnp.dot(student_input, student_gate, preferred_element_type=jnp.float32)
    up_part = jnp.dot(student_input, student_up, preferred_element_type=jnp.float32)
    gate, up = side_by_side((gate_part, up_part), "st", 0, 1)
    hidden_share = (jax.nn.silu(gate) * up).astype(jnp.bfloat16)
    hidden = gathered_copies(hidden_share, "st", 0)
    down_sum = sum_by_parts(
        jnp.dot(hidden, student_down, preferred_element_type=jnp.float32), ("tr", "tc")
    )
    features = (student_stream.astype(jnp.float32) + down_sum).astype(jnp.bfloat16)
    partial_term = jnp.dot(features, head, preferred_element_type=jnp.float32) - teacher_term
    error_share = sent_and_summed(partial_term, "st", 0)
    count = error_share.shape[0]
    residual_share = lax.dynamic_slice_in_dim(
        teacher_residual, lax.axis_index("st") * count, count, 0
    )
    signal_share = ((error_share - residual_share.astype(jnp.float32)) * loss_scale).astype(
        jnp.bfloat16
    )
    signal = gathered_copies(signal_share, "st", 0)
    grad_head = contract_rows(features, signal)
    feature_grad = sum_by_parts(contract_cols(signal, head), ("tr", "tc")).astype(jnp.bfloat16)
    grad_down = contract_rows(hidden, feature_grad)
    hidden_part = contract_cols(feature_grad, student_down)
    hidden_grad = sent_and_summed(hidden_part, "st", 0)
    gate_share, up_share = activation_grads(hidden_grad, gate, up)
    gate_signal, up_signal = sent_together((gate_share, up_share), "st", 0, 1)
    grad_gate = contract_rows(student_input, gate_signal)
    grad_up = contract_rows(student_input, up_signal)
    return (grad_gate, grad_up, grad_down, grad_head)


def solution(mesh):
    in_specs = (
        P(None, "st"),
        P(None, ("tr", "tc")),
        P("st", ("tr", "tc")),
        P(None, "st"),
        P(None, "st"),
        P("st", ("tr", "tc")),
        P("st", ("tr", "tc")),
        P(("tr", "tc"), "st"),
        P("st", ("tr", "tc")),
    )
    out_specs = (
        P("st", ("tr", "tc")),
        P("st", ("tr", "tc")),
        P(("tr", "tc"), "st"),
        P("st", ("tr", "tc")),
    )
    return jax.shard_map(body, mesh=mesh, in_specs=in_specs, out_specs=out_specs, check_vma=False)
```

profile of v0, /device:TPU:8, one launch (start us, length us, event | category | flops | bytes accessed | tf_op | source)
XLA Modules:
  0.0 241.1 jit_solution(7188082832987081438)
XLA Ops:
  0.6 0.0 copy-start
  0.6 1.5 fusion.12
  2.2 1.4 fusion.13
  3.6 0.1 pad_maximum_fusion
  3.7 53.0 %all_to_all.45 = f32[16,16,1792]{2,1,0:T(8,128)} all-to-all(f32[16,16,1792]{2,1,0:T(8,128)S(1)} %bitcast.38), channel_id=1, replica_groups=mesh['tr'=4,'tc'=4,'st'=16] {'st'}, dimensions={0} | all-to-all | bytes 3670016 | tf_op jit(solution)/shard_map/all_to_all | solution.py:16
  56.7 0.0 copy-start.2
  56.7 1.7 reduce_sum.45
  58.3 0.0 copy-start.5
  58.4 0.6 copy-done.5
  59.0 17.7 %all_to_all.46 = bf16[16,16,896]{2,1,0:T(8,128)(2,1)S(1)} all-to-all(bf16[16,16,896]{2,1,0:T(8,128)(2,1)S(1)} %broadcast_in_dim.8), channel_id=1, replica_groups=mesh['tr'=4,'tc'=4,'st'=16] {'st'}, dimensions={0} | all-to-all | bytes 917504 | tf_op jit(solution)/shard_map/all_to_all | solution.py:37
  76.7 0.0 copy-done.2
  76.7 0.3 fusion.4
  77.0 15.1 %all_to_all.47 = f32[16,16,256]{2,1,0:T(8,128)S(1)} all-to-all(f32[16,16,256]{2,1,0:T(8,128)S(1)} %fusion.4), channel_id=1, replica_groups=mesh['tr'=4,'tc'=4,'st'=16] {'tr','tc'}, dimensions={0} | all-to-all | bytes 524288 | tf_op jit(solution)/shard_map/all_to_all | solution.py:16
  92.1 0.7 broadcast_in_dim.9
  92.9 4.2 %all-to-all-start.3 = ((f32[16,16,256]{2,1,0:T(8,128)}), f32[16,16,256]{2,1,0:T(8,128)}, u32[]{:S(2)}, u32[]{:S(2)}) async-start(f32[16,16,256]{2,1,0:T(8,128)} %broadcast_in_dim.9), calls=%async_computation.3 | async-start | bytes 524288 | tf_op jit(solution)/shard_map/all_to_all | solution.py:37
  97.1 0.0 copy-done
  97.1 0.0 copy-start.4
  97.1 1.9 fusion.14
  99.0 7.3 %all-to-all-done.3 = f32[16,16,256]{2,1,0:T(8,128)} async-done(((f32[16,16,256]{2,1,0:T(8,128)}), f32[16,16,256]{2,1,0:T(8,128)}, u32[]{:S(2)}, u32[]{:S(2)}) %all-to-all-start.3) | async-done | bytes 262176 | tf_op jit(solution)/shard_map/all_to_all | solution.py:37
  106.3 1.0 fusion.8
  107.3 0.0 copy-done.4
  107.3 0.0 copy-start.3
  107.3 1.0 convolution_subtract_fusion
  108.3 0.0 copy-done.3
  108.3 6.0 %all-to-all-start.4 = ((f32[16,16,512]{2,1,0:T(8,128)}), f32[16,16,512]{2,1,0:T(8,128)S(1)}, u32[]{:S(2)}, u32[]{:S(2)}) async-start(f32[16,16,512]{2,1,0:T(8,128)} %bitcast.3), calls=%async_computation.4 | async-start | bytes 1048576 | tf_op jit(solution)/shard_map/all_to_all | solution.py:16
  114.4 14.9 %all-to-all-done.4 = f32[16,16,512]{2,1,0:T(8,128)S(1)} async-done(((f32[16,16,512]{2,1,0:T(8,128)}), f32[16,16,512]{2,1,0:T(8,128)S(1)}, u32[]{:S(2)}, u32[]{:S(2)}) %all-to-all-start.4) | async-done | bytes 524320 | tf_op jit(solution)/shard_map/all_to_all | solution.py:16
  129.2 0.6 reduce_sum.47
  129.9 0.8 multiply_convert_fusion.3
  130.7 14.8 %all_to_all.48 = bf16[16,16,512]{2,1,0:T(8,128)(2,1)S(1)} all-to-all(bf16[16,16,512]{2,1,0:T(8,128)(2,1)S(1)} %broadcast_in_dim.10), channel_id=1, replica_groups=mesh['tr'=4,'tc'=4,'st'=16] {'st'}, dimensions={0} | all-to-all | bytes 524288 | tf_op jit(solution)/shard_map/all_to_all | solution.py:37
  145.4 0.3 fusion.6
  145.7 11.9 %all_to_all.49 = f32[16,16,256]{2,1,0:T(8,128)S(1)} all-to-all(f32[16,16,256]{2,1,0:T(8,128)S(1)} %fusion.6), channel_id=1, replica_groups=mesh['tr'=4,'tc'=4,'st'=16] {'tr','tc'}, dimensions={0} | all-to-all | bytes 524288 | tf_op jit(solution)/shard_map/all_to_all | solution.py:16
  157.7 10.6 %all_to_all.50 = bf16[16,16,256]{2,1,0:T(8,128)(2,1)S(1)} all-to-all(bf16[16,16,256]{2,1,0:T(8,128)(2,1)S(1)} %broadcast_in_dim.11), channel_id=1, replica_groups=mesh['tr'=4,'tc'=4,'st'=16] {'tr','tc'}, dimensions={0} | all-to-all | bytes 262144 | tf_op jit(solution)/shard_map/all_to_all | solution.py:37
  168.3 1.3 fusion.2
  169.5 0.0 copy-done.7
  169.5 5.7 %all-to-all-start.8 = ((f32[16,16,896]{2,1,0:T(8,128)}), f32[16,16,896]{2,1,0:T(8,128)S(1)}, u32[]{:S(2)}, u32[]{:S(2)}) async-start(f32[16,16,896]{2,1,0:T(8,128)} %fusion.2), calls=%async_computation.8 | async-start | bytes 1835008 | tf_op jit(solution)/shard_map/all_to_all | solution.py:16
  175.2 1.9 fusion.15
  177.2 0.0 copy-start.6
  177.2 2.2 convolution_bitcast_fusion.2
  179.4 0.0 copy-start.1
  179.4 19.2 %all-to-all-done.8 = f32[16,16,896]{2,1,0:T(8,128)S(1)} async-done(((f32[16,16,896]{2,1,0:T(8,128)}), f32[16,16,896]{2,1,0:T(8,128)S(1)}, u32[]{:S(2)}, u32[]{:S(2)}) %all-to-all-start.8) | async-done | bytes 917536 | tf_op jit(solution)/shard_map/all_to_all | solution.py:16
  198.6 0.1 reduce_sum.49
  198.6 0.0 copy-done.6
  198.7 37.2 %all_gather.3 = bf16[256,1792]{1,0:T(8,128)(2,1)S(1)} all-gather(bf16[16,1792]{1,0:T(8,128)(2,1)S(1)} %pad_maximum_fusion.1), channel_id=1, replica_groups=mesh['tr'=4,'tc'=4,'st'=16] {'st'}, dimensions={0}, use_global_device_ids=true | all-gather | bytes 974848 | tf_op jit(solution)/shard_map/all_gather | solution.py:64
  235.9 0.0 copy-done.1
  235.9 1.3 convolution_bitcast_fusion.1
  237.2 0.3 convolution_bitcast_fusion
  237.5 2.4 copy.13
  239.9 1.2 copy.14
  (9 shorter events, 0.2 us)
Async XLA Ops:
  0.6 96.4 %copy-start = (bf16[1792,512]{1,0:T(8,128)(2,1)S(1)}, bf16[1792,512]{1,0:T(8,128)(2,1)}, u32[]{:S(2)}) copy-start(bf16[1792,512]{1,0:T(8,128)(2,1)} %param.11) | copy-start | bytes 5505028
  56.7 20.0 %copy-start.2 = (bf16[896,256]{1,0:T(8,128)(2,1)S(1)}, bf16[896,256]{1,0:T(8,128)(2,1)}, u32[]{:S(2)}) copy-start(bf16[896,256]{1,0:T(8,128)(2,1)} %param.16) | copy-start | bytes 1376260
  58.3 0.7 copy-start.5
  92.9 13.4 %all-to-all-start.3 = ((f32[16,16,256]{2,1,0:T(8,128)}), f32[16,16,256]{2,1,0:T(8,128)}, u32[]{:S(2)}, u32[]{:S(2)}) async-start(f32[16,16,256]{2,1,0:T(8,128)} %broadcast_in_dim.9), calls=%async_computation.3 | async-start | bytes 524288 | tf_op jit(solution)/shard_map/all_to_all | solution.py:37
  97.1 10.2 %copy-start.4 = (bf16[256,512]{1,0:T(8,128)(2,1)S(1)}, bf16[256,512]{1,0:T(8,128)(2,1)}, u32[]{:S(2)}) copy-start(bf16[256,512]{1,0:T(8,128)(2,1)} %param.17) | copy-start | bytes 786436
  107.3 1.0 copy-start.3
  108.3 20.9 %all-to-all-start.4 = ((f32[16,16,512]{2,1,0:T(8,128)}), f32[16,16,512]{2,1,0:T(8,128)S(1)}, u32[]{:S(2)}, u32[]{:S(2)}) async-start(f32[16,16,512]{2,1,0:T(8,128)} %bitcast.3), calls=%async_computation.4 | async-start | bytes 1048576 | tf_op jit(solution)/shard_map/all_to_all | solution.py:16
  168.3 1.3 copy-start.7
  169.5 29.0 %all-to-all-start.8 = ((f32[16,16,896]{2,1,0:T(8,128)}), f32[16,16,896]{2,1,0:T(8,128)S(1)}, u32[]{:S(2)}, u32[]{:S(2)}) async-start(f32[16,16,896]{2,1,0:T(8,128)} %fusion.2), calls=%async_computation.8 | async-start | bytes 1835008 | tf_op jit(solution)/shard_map/all_to_all | solution.py:16
  177.2 21.4 %copy-start.6 = (f32[16,1792]{1,0:T(8,128)S(1)}, f32[16,1792]{1,0:T(8,128)}, u32[]{:S(2)}) copy-start(f32[16,1792]{1,0:T(8,128)} %copy-done.5) | copy-start | bytes 344068
  179.4 56.5 %copy-start.1 = (bf16[256,256]{1,0:T(8,128)(2,1)S(1)}, bf16[256,256]{1,0:T(8,128)(2,1)}, u32[]{:S(2)}) copy-start(bf16[256,256]{1,0:T(8,128)(2,1)} %param.12) | copy-start | bytes 393220
where the time goes:
time: 242 us; the launch traced here: 241 us
  blocking collectives  160 us (66%)
  waiting for transfers between devices  41.3 us (17%)
  starting transfers between devices  16 us (7%)
  matrix products  13.3 us (5%)
  local copies, waits for them, and re-layouts  5.08 us (2%)
  other arithmetic  4.37 us (2%)
    all_to_all x3, blocking collectives, sent_and_summed(): lax.all_to_all(split_up(array, dim, length), axis, 0, 0, tiled=True)  80 us
    all_to_all x3, blocking collectives, copy_for_each(): lax.all_to_all(jnp.broadcast_to(array[None], (length, *array.shape)), axi...  43.1 us
    all_gather x1, blocking collectives, sent_together(): lax.all_gather(both, axis, axis=dim, tiled=True)  37.2 us
    all_to_all x2, waiting for transfers between devices, sent_and_summed(): lax.all_to_all(split_up(array, dim, length), axis, 0, 0, tiled=True)  34 us
    all_to_all x2, starting transfers between devices, sent_and_summed(): lax.all_to_all(split_up(array, dim, length), axis, 0, 0, tiled=True)  11.8 us
    all_to_all x1, waiting for transfers between devices, copy_for_each(): lax.all_to_all(jnp.broadcast_to(array[None], (length, *array.shape)), axi...  7.3 us
    dot_general x4, matrix products, contract_rows(): lax.dot_general(left, right, (((0,), (0,)), ((), ())), preferred_element_...  5.74 us
  transfers between devices with their start and end apart: 3, of which 3 were waited for; matrix products, arithmetic and copies ran while one was open for 2% of the time, Pallas kernels for 0%

commit v1 on v0

v1 whole, which is shorter than its diff:
```python
import functools
import math

import jax
import jax.numpy as jnp
from jax import lax
from jax.experimental import pallas as pl
from jax.experimental.pallas import tpu as pltpu
from jax.sharding import PartitionSpec as P

BF = jnp.bfloat16
F32 = jnp.float32
MESH = pl.DeviceIdType.MESH
N = 16
OTHERS = N - 1


def dot(a, b):
    return jnp.dot(a, b, preferred_element_type=F32)


def dot_cols(a, b):
    return lax.dot_general(a, b, (((1,), (1,)), ((), ())), preferred_element_type=F32)


def contract_rows(left, right):
    return lax.dot_general(
        left, right, (((0,), (0,)), ((), ())), preferred_element_type=F32
    )


def kernel(
    tc_size,
    th, res, td, xin, stream, wg, wu, wd, hd,
    o_hid, o_feat, o_sig, o_fg, o_gs, o_us,
    v_th, v_res, v_td, v_x, v_stream, v_wg, v_wu, v_wd, v_hd,
    f1, p1, r1, g2s, g2, f3, p3, r3, g3s, g3, f4, p4, r4, g5s, g5,
    f6, p6, r6, g6s, g6, f7, p7, r7, g8as, g8a, g8bs, g8b,
    gate_ref, up_ref,
    load_sem, out_sem, send_sem, recv_sem,
):
    tokens = p1.shape[0]
    rows = tokens // N
    fs = wg.shape[1]
    st = lax.axis_index("st")
    grp = lax.axis_index("tr") * tc_size + lax.axis_index("tc")

    def st_peer(k):
        p = lax.rem(st + k, N)
        return p, {"st": p}

    def grp_peer(k):
        p = lax.rem(grp + k, N)
        return p, {"tr": p // tc_size, "tc": lax.rem(p, tc_size)}

    def at_rows(ref, i):
        return ref.at[pl.ds(pl.multiple_of(i * rows, rows), rows), :]

    loads = [
        pltpu.make_async_copy(src, dst, load_sem.at[i])
        for i, (src, dst) in enumerate(
            [
                (xin, v_x), (wg, v_wg), (wu, v_wu), (th, v_th), (td, v_td),
                (wd, v_wd), (hd, v_hd), (at_rows(stream, grp), v_stream),
                (at_rows(res, st), v_res),
            ]
        )
    ]
    for c in loads:
        c.start()

    barrier = pltpu.get_barrier_semaphore()

    def greet(k, carry):
        for peer in (st_peer, grp_peer):
            pl.semaphore_signal(barrier, inc=1, device_id=peer(k)[1], device_id_type=MESH)
        return carry

    lax.fori_loop(1, N, greet, 0)

    def scatter(i, peer, part, slots):
        def one(k, carry):
            p, device = peer(k)
            pltpu.make_async_remote_copy(
                src_ref=at_rows(part, p), dst_ref=slots.at[OTHERS - k],
                send_sem=send_sem.at[i], recv_sem=recv_sem.at[i],
                device_id=device, device_id_type=MESH,
            ).start()
            return carry

        lax.fori_loop(1, N, one, 0)

    def arrived(i, slots):
        pltpu.make_async_copy(slots, slots, recv_sem.at[i]).wait()

    def summed(i, own, slots):
        arrived(i, slots)
        total = own
        for k in range(OTHERS):
            total = total + slots[k].astype(F32)
        return total

    def spread(i, peer, share, whole, me):
        def one(k, carry):
            device = peer(k)[1]
            pltpu.make_async_remote_copy(
                src_ref=share, dst_ref=at_rows(whole, me),
                send_sem=send_sem.at[i], recv_sem=recv_sem.at[i],
                device_id=device, device_id_type=MESH,
            ).start()
            return carry

        lax.fori_loop(1, N, one, 0)

    def gathered(i, whole):
        most = whole.at[pl.ds(0, OTHERS * rows), :]
        pltpu.make_async_copy(most, most, recv_sem.at[i]).wait()

    def sent(i, like):
        most = like.at[pl.ds(0, OTHERS * rows), :]
        pltpu.make_async_copy(most, most, send_sem.at[i]).wait()

    def put(ref, i, value):
        ref[pl.ds(pl.multiple_of(i * rows, rows), rows), :] = value

    def get(ref, i):
        return ref[pl.ds(pl.multiple_of(i * rows, rows), rows), :]

    outs = []

    def out(src, dst):
        c = pltpu.make_async_copy(src, dst, out_sem.at[len(outs)])
        c.start()
        outs.append(c)

    for c in loads[:3]:
        c.wait()
    for w, at in ((v_wg, 0), (v_wu, fs)):
        part = dot(v_x[...], w[...])
        f1[:, pl.ds(at, fs)] = part
        p1[:, pl.ds(at, fs)] = part.astype(BF)
    pl.semaphore_wait(barrier, 2 * OTHERS)
    scatter(0, st_peer, p1, r1)
    for c in loads[3:]:
        c.wait()
    f4[...] = dot(v_th[...], v_td[...])
    both = summed(0, get(f1, st), r1)
    gate, up = both[:, :fs], both[:, fs:]
    gate_ref[...] = gate
    up_ref[...] = up
    share = (gate * jax.nn.sigmoid(gate) * up).astype(BF)
    g2s[...] = share
    spread(1, st_peer, g2s, g2, st)
    put(g2, st, share)
    gathered(1, g2)
    part = dot(g2[...], v_wd[...])
    f3[...] = part
    p3[...] = part.astype(BF)
    scatter(2, grp_peer, p3, r3)
    out(g2, o_hid)
    total = summed(2, get(f3, grp), r3)
    share = (v_stream[...].astype(F32) + total).astype(BF)
    g3s[...] = share
    spread(3, grp_peer, g3s, g3, grp)
    put(g3, grp, share)
    gathered(3, g3)
    part = dot(g3[...], v_hd[...]) - f4[...]
    f4[...] = part
    p4[...] = part.astype(BF)
    scatter(4, st_peer, p4, r4)
    out(g3, o_feat)
    total = summed(4, get(f4, st), r4)
    share = ((total - v_res[...].astype(F32)) * (1.0 / math.sqrt(tokens))).astype(BF)
    g5s[...] = share
    spread(5, st_peer, g5s, g5, st)
    put(g5, st, share)
    gathered(5, g5)
    part = dot_cols(g5[...], v_hd[...])
    f6[...] = part
    p6[...] = part.astype(BF)
    scatter(6, grp_peer, p6, r6)
    out(g5, o_sig)
    share = summed(6, get(f6, grp), r6).astype(BF)
    g6s[...] = share
    spread(7, grp_peer, g6s, g6, grp)
    put(g6, grp, share)
    gathered(7, g6)
    part = dot_cols(g6[...], v_wd[...])
    f7[...] = part
    p7[...] = part.astype(BF)
    scatter(8, st_peer, p7, r7)
    out(g6, o_fg)
    gate, up = gate_ref[...], up_ref[...]
    sigma = jax.nn.sigmoid(gate)
    grad = summed(8, get(f7, st), r7)
    gate_share = (grad * up * (sigma * (1.0 + gate * (1.0 - sigma)))).astype(BF)
    up_share = (grad * (gate * sigma)).astype(BF)
    g8as[...] = gate_share
    spread(9, st_peer, g8as, g8a, st)
    g8bs[...] = up_share
    spread(10, st_peer, g8bs, g8b, st)
    put(g8a, st, gate_share)
    put(g8b, st, up_share)
    gathered(9, g8a)
    out(g8a, o_gs)
    gathered(10, g8b)
    out(g8b, o_us)
    for i, like in enumerate((p1, g2, p3, g3, p4, g5, p6, g6, p7, g8a, g8b)):
        sent(i, like)
    for c in outs:
        c.wait()


def body(
    teacher_hidden, teacher_residual, teacher_down, student_input, student_stream,
    student_gate, student_up, student_down, head,
):
    tokens, ds = student_input.shape
    fs = student_gate.shape[1]
    dt = head.shape[1]
    rows = tokens // N
    arguments = (
        teacher_hidden, teacher_residual, teacher_down, student_input, student_stream,
        student_gate, student_up, student_down, head,
    )
    vm = lambda shape, dtype: pltpu.VMEM(shape, dtype)

    def reduce_bufs(cols):
        return [vm((tokens, cols), F32), vm((tokens, cols), BF), vm((OTHERS, rows, cols), BF)]

    def gather_bufs(cols):
        return [vm((rows, cols), BF), vm((tokens, cols), BF)]

    staged = [
        vm((rows, a.shape[1]), a.dtype) if i in (1, 4) else vm(a.shape, a.dtype)
        for i, a in enumerate(arguments)
    ]
    scratch = (
        staged
        + reduce_bufs(2 * fs) + gather_bufs(fs)
        + reduce_bufs(ds) + gather_bufs(ds)
        + reduce_bufs(dt) + gather_bufs(dt)
        + reduce_bufs(ds) + gather_bufs(ds)
        + reduce_bufs(fs) + gather_bufs(fs) + gather_bufs(fs)
        + [vm((rows, fs), F32), vm((rows, fs), F32)]
        + [
            pltpu.SemaphoreType.DMA((9,)),
            pltpu.SemaphoreType.DMA((6,)),
            pltpu.SemaphoreType.DMA((11,)),
            pltpu.SemaphoreType.DMA((11,)),
        ]
    )
    shapes = [(tokens, c) for c in (fs, ds, dt, ds, fs, fs)]
    hidden, features, signal, feature_grad, gate_signal, up_signal = pl.pallas_call(
        functools.partial(kernel, lax.axis_size("tc")),
        out_shape=[jax.ShapeDtypeStruct(s, BF) for s in shapes],
        in_specs=[pl.BlockSpec(memory_space=pl.ANY)] * 9,
        out_specs=[pl.BlockSpec(memory_space=pl.ANY)] * 6,
        scratch_shapes=scratch,
        compiler_params=pltpu.CompilerParams(
            collective_id=0, has_side_effects=True, vmem_limit_bytes=56 << 20
        ),
        name="chain",
    )(*arguments)
    return (
        contract_rows(student_input, gate_signal),
        contract_rows(student_input, up_signal),
        contract_rows(hidden, feature_grad),
        contract_rows(features, signal),
    )


def solution(mesh):
    in_specs = (
        P(None, "st"),
        P(None, ("tr", "tc")),
        P("st", ("tr", "tc")),
        P(None, "st"),
        P(None, "st"),
        P("st", ("tr", "tc")),
        P("st", ("tr", "tc")),
        P(("tr", "tc"), "st"),
        P("st", ("tr", "tc")),
    )
    out_specs = (
        P("st", ("tr", "tc")),
        P("st", ("tr", "tc")),
        P(("tr", "tc"), "st"),
        P("st", ("tr", "tc")),
    )
    return jax.shard_map(body, mesh=mesh, in_specs=in_specs, out_specs=out_specs, check_vma=False)
```

time: 242 us -> 129 us (0.53)
  blocking collectives: 160 us -> 0 us
  Pallas kernels: 0 us -> 121 us
  waiting for transfers between devices: 41.3 us -> 0 us
  starting transfers between devices: 16 us -> 0 us
  matrix products: 13.3 us -> 4.04 us
  other arithmetic: 4.37 us -> 0 us
  local copies, waits for them, and re-layouts: 5.08 us -> 2.48 us
    all_to_all x6 -> x0, blocking collectives: 123 us -> none  [the longest x3 80 us: sent_and_summed(): lax.all_to_all(split_up(array, dim, length), axis, 0, 0, tiled=True)]
    pallas_call x0 -> x1, Pallas kernels: none -> 121 us  [body(): pl.pallas_call(functools.partial(kernel, lax.axis_size('tc')), out_shape=...]
    all_to_all x3 -> x0, waiting for transfers between devices: 41.3 us -> none  [the longest x2 34 us: sent_and_summed(): lax.all_to_all(split_up(array, dim, length), axis, 0, 0, tiled=True)]
    all_gather x1 -> x0, blocking collectives: 37.2 us -> none  [sent_together(): lax.all_gather(both, axis, axis=dim, tiled=True)]
    all_to_all x3 -> x0, starting transfers between devices: 16 us -> none  [the longest x2 11.8 us: sent_and_summed(): lax.all_to_all(split_up(array, dim, length), axis, 0, 0, tiled=True)]
    dot_general x7 -> x0, matrix products: 7.59 us -> none  [the longest x1 1.85 us: body(): jnp.dot(teacher_hidden, teacher_down, preferred_element_type=jnp.float32)]
  transfers between devices with their start and end apart: 3 -> 0, of which waited for: 3 -> 0; matrix products, arithmetic and copies ran while one was open for 2% -> 0% of each run, Pallas kernels for 0% -> 0%
where the time goes in v1:
time: 129 us; the launch traced here: 128 us
  Pallas kernels  121 us (94%)
  matrix products  4.04 us (3%)
  local copies, waits for them, and re-layouts  2.48 us (2%)
    pallas_call x1, Pallas kernels, body(): pl.pallas_call(functools.partial(kernel, lax.axis_size('tc')), out_shape=...  121 us
    dot_general x4, matrix products, contract_rows(): lax.dot_general(left, right, (((0,), (0,)), ((), ())), preferred_element_...  4.04 us

profile of v1, /device:TPU:8, one launch (start us, length us, event | category | flops | bytes accessed | tf_op | source)
XLA Modules:
  0.0 128.2 jit_solution(6896171343982916820)
XLA Ops:
  0.6 0.0 copy-start
  0.6 121.0 %chain.1 = (bf16[256,896]{1,0:T(8,128)(2,1)}, bf16[256,256]{1,0:T(8,128)(2,1)}, bf16[256,512]{1,0:T(8,128)(2,1)}, bf16[256,256]{1,0:T(8,128)(2,1)}, bf16[256,896]{1,0:T(8,128)(2,1)}, /*index=5*/bf16[256,896]{1,0:T(8,128)(2,1)}) custom-call(bf16[256,1792]{1,0:T(8,128)(2,1)} %th.1, bf16[256,512]{1,0:T(8,128)(2,1)} %res.1, bf16[1792,512]{1,0:T(8,128)(2,1)} %td.1, ...), custom_call_target="tpu_custom_call" | custom-call | tf_op jit(solution)/shard_map/chain/pallas_call | solution.py:254
  121.7 0.0 copy-start.2
  121.7 0.0 copy-done
  121.7 1.4 %convolution_bitcast_fusion.1 = f32[256,896]{0,1:T(8,128)S(1)} fusion(bf16[256,896]{1,0:T(8,128)(2,1)} %get-tuple-element.10, bf16[256,256]{1,0:T(8,128)(2,1)S(1)} %copy-done), kind=kOutput, calls=%fused_computation.1 | convolution fusion | flops 117440512 | bytes 1507328 | tf_op jit(solution)/shard_map/dot_general | solution.py:27
  123.1 1.2 copy.13
  124.3 0.0 copy-start.1
  124.3 0.0 copy-start.5
  124.3 0.0 copy-done.2
  124.3 0.3 convolution_bitcast_fusion
  124.7 0.0 copy-start.3
  124.7 0.0 copy-start.4
  124.7 1.2 copy.14
  125.9 0.0 copy-done.1
  125.9 0.0 copy-done.5
  125.9 1.3 fusion
  127.2 0.0 copy-done.3
  127.2 0.0 copy-done.4
  127.2 1.0 fusion.1
Async XLA Ops:
  0.6 121.0 %copy-start = (bf16[256,256]{1,0:T(8,128)(2,1)S(1)}, bf16[256,256]{1,0:T(8,128)(2,1)}, u32[]{:S(2)}) copy-start(bf16[256,256]{1,0:T(8,128)(2,1)} %xin.1) | copy-start | bytes 393220
  121.7 2.7 %copy-start.2 = (bf16[256,896]{1,0:T(8,128)(2,1)S(1)}, bf16[256,896]{1,0:T(8,128)(2,1)}, u32[]{:S(2)}) copy-start(bf16[256,896]{1,0:T(8,128)(2,1)} %get-tuple-element.11) | copy-start | bytes 1376260
  124.3 1.6 %copy-start.1 = (bf16[256,896]{1,0:T(8,128)(2,1)S(1)}, bf16[256,896]{1,0:T(8,128)(2,1)}, u32[]{:S(2)}) copy-start(bf16[256,896]{1,0:T(8,128)(2,1)} %get-tuple-element.12) | copy-start | bytes 1376260
  124.3 1.6 %copy-start.5 = (bf16[256,256]{1,0:T(8,128)(2,1)S(1)}, bf16[256,256]{1,0:T(8,128)(2,1)}, u32[]{:S(2)}) copy-start(bf16[256,256]{1,0:T(8,128)(2,1)} %get-tuple-element.13) | copy-start | bytes 393220
  124.7 2.5 %copy-start.3 = (bf16[256,512]{1,0:T(8,128)(2,1)S(1)}, bf16[256,512]{1,0:T(8,128)(2,1)}, u32[]{:S(2)}) copy-start(bf16[256,512]{1,0:T(8,128)(2,1)} %get-tuple-element.15) | copy-start | bytes 786436
  124.7 2.5 %copy-start.4 = (bf16[256,256]{1,0:T(8,128)(2,1)S(1)}, bf16[256,256]{1,0:T(8,128)(2,1)}, u32[]{:S(2)}) copy-start(bf16[256,256]{1,0:T(8,128)(2,1)} %get-tuple-element.14) | copy-start | bytes 393220

commit v2 on v1

--- a/solution.py
+++ b/solution.py
@@ -35,8 +35,8 @@
     o_hid, o_feat, o_sig, o_fg, o_gs, o_us,
     v_th, v_res, v_td, v_x, v_stream, v_wg, v_wu, v_wd, v_hd,
     f1, p1, r1, g2s, g2, f3, p3, r3, g3s, g3, f4, p4, r4, g5s, g5,
-    f6, p6, r6, g6s, g6, f7, p7, r7, g8as, g8a, g8bs, g8b,
-    gate_ref, up_ref,
+    f6, p6, r6, g6s, g6, f7, p7, r7, g8s, g8,
+    gates, gate_ref, ups, up_ref, by_gate, by_up, s_gate, s_up,
     load_sem, out_sem, send_sem, recv_sem,
 ):
     tokens = p1.shape[0]
@@ -146,17 +146,20 @@
     f4[...] = dot(v_th[...], v_td[...])
     both = summed(0, get(f1, st), r1)
     gate, up = both[:, :fs], both[:, fs:]
-    gate_ref[...] = gate
-    up_ref[...] = up
+    gates[...] = gate.astype(BF)
+    ups[...] = up.astype(BF)
     share = (gate * jax.nn.sigmoid(gate) * up).astype(BF)
     g2s[...] = share
     spread(1, st_peer, g2s, g2, st)
     put(g2, st, share)
+    put(gate_ref, st, gates[...])
+    put(up_ref, st, ups[...])
     gathered(1, g2)
     part = dot(g2[...], v_wd[...])
     f3[...] = part
     p3[...] = part.astype(BF)
     scatter(2, grp_peer, p3, r3)
+    spread(9, st_peer, gates, gate_ref, st)
     out(g2, o_hid)
     total = summed(2, get(f3, grp), r3)
     share = (v_stream[...].astype(F32) + total).astype(BF)
@@ -179,6 +182,7 @@
     f6[...] = part
     p6[...] = part.astype(BF)
     scatter(6, grp_peer, p6, r6)
+    spread(10, st_peer, ups, up_ref, st)
     out(g5, o_sig)
     share = summed(6, get(f6, grp), r6).astype(BF)
     g6s[...] = share
@@ -190,24 +194,57 @@
     p7[...] = part.astype(BF)
     scatter(8, st_peer, p7, r7)
     out(g6, o_fg)
-    gate, up = gate_ref[...], up_ref[...]
+    gathered(9, gate_ref)
+    gathered(10, up_ref)
+    gate = gate_ref[...].astype(F32)
     sigma = jax.nn.sigmoid(gate)
-    grad = summed(8, get(f7, st), r7)
-    gate_share = (grad * up * (sigma * (1.0 + gate * (1.0 - sigma)))).astype(BF)
-    up_share = (grad * (gate * sigma)).astype(BF)
-    g8as[...] = gate_share
-    spread(9, st_peer, g8as, g8a, st)
-    g8bs[...] = up_share
-    spread(10, st_peer, g8bs, g8b, st)
-    put(g8a, st, gate_share)
-    put(g8b, st, up_share)
-    gathered(9, g8a)
-    out(g8a, o_gs)
-    gathered(10, g8b)
-    out(g8b, o_us)
-    for i, like in enumerate((p1, g2, p3, g3, p4, g5, p6, g6, p7, g8a, g8b)):
+    by_gate[...] = up_ref[...].astype(F32) * (sigma * (1.0 + gate * (1.0 - sigma)))
+    by_up[...] = gate * sigma
+    share = summed(8, get(f7, st), r7).astype(BF)
+    g8s[...] = share
+    spread(11, st_peer, g8s, g8, st)
+    put(g8, st, share)
+    gathered(11, g8)
+    grad = g8[...].astype(F32)
+    s_gate[...] = (grad * by_gate[...]).astype(BF)
+    out(s_gate, o_gs)
+    s_up[...] = (grad * by_up[...]).astype(BF)
+    out(s_up, o_us)
+    for i, like in enumerate((p1, g2, p3, g3, p4, g5, p6, g6, p7, gate_ref, up_ref, g8)):
         sent(i, like)
     for c in outs:
+        c.wait()
+
+
+def gradients(
+    x, gs, us, hid, fg, feat, sig, o_gate, o_up, o_down, o_head,
+    v_x, v_gs, v_us, v_hid, v_fg, v_feat, v_sig, r_gate, r_up, r_down, r_head,
+    load_sem, out_sem,
+):
+    pairs = [
+        (feat, v_feat), (sig, v_sig), (hid, v_hid), (fg, v_fg),
+        (x, v_x), (gs, v_gs), (us, v_us),
+    ]
+    loads = [
+        pltpu.make_async_copy(src, dst, load_sem.at[i]) for i, (src, dst) in enumerate(pairs)
+    ]
+    for c in loads:
+        c.start()
+    stores = []
+    for need, left, right, result, dest in (
+        (2, v_feat, v_sig, r_head, o_head),
+        (2, v_hid, v_fg, r_down, o_down),
+        (2, v_x, v_gs, r_gate, o_gate),
+        (1, v_x, v_us, r_up, o_up),
+    ):
+        for c in loads[:need]:
+            c.wait()
+        loads = loads[need:]
+        result[...] = contract_rows(left[...], right[...])
+        c = pltpu.make_async_copy(result, dest, out_sem.at[len(stores)])
+        c.start()
+        stores.append(c)
+    for c in stores:
         c.wait()
 
 
@@ -241,13 +278,15 @@
         + reduce_bufs(ds) + gather_bufs(ds)
         + reduce_bufs(dt) + gather_bufs(dt)
         + reduce_bufs(ds) + gather_bufs(ds)
-        + reduce_bufs(fs) + gather_bufs(fs) + gather_bufs(fs)
-        + [vm((rows, fs), F32), vm((rows, fs), F32)]
+        + reduce_bufs(fs) + gather_bufs(fs)
+        + gather_bufs(fs) + gather_bufs(fs)
+        + [vm((tokens, fs), F32)] * 2
+        + [vm((tokens, fs), BF)] * 2
         + [
             pltpu.SemaphoreType.DMA((9,)),
             pltpu.SemaphoreType.DMA((6,)),
-            pltpu.SemaphoreType.DMA((11,)),
-            pltpu.SemaphoreType.DMA((11,)),
+            pltpu.SemaphoreType.DMA((12,)),
+            pltpu.SemaphoreType.DMA((12,)),
         ]
     )
     shapes = [(tokens, c) for c in (fs, ds, dt, ds, fs, fs)]
@@ -258,16 +297,22 @@
         out_specs=[pl.BlockSpec(memory_space=pl.ANY)] * 6,
         scratch_shapes=scratch,
         compiler_params=pltpu.CompilerParams(
-            collective_id=0, has_side_effects=True, vmem_limit_bytes=56 << 20
+            collective_id=0, has_side_effects=True
         ),
         name="chain",
     )(*arguments)
-    return (
-        contract_rows(student_input, gate_signal),
-        contract_rows(student_input, up_signal),
-        contract_rows(hidden, feature_grad),
-        contract_rows(features, signal),
-    )
+    operands = (student_input, gate_signal, up_signal, hidden, feature_grad, features, signal)
+    results = [(ds, fs), (ds, fs), (fs, ds), (ds, dt)]
+    return pl.pallas_call(
+        gradients,
+        out_shape=[jax.ShapeDtypeStruct(s, F32) for s in results],
+        in_specs=[pl.BlockSpec(memory_space=pl.ANY)] * 7,
+        out_specs=[pl.BlockSpec(memory_space=pl.ANY)] * 4,
+        scratch_shapes=[vm(a.shape, a.dtype) for a in operands]
+        + [vm(s, F32) for s in results]
+        + [pltpu.SemaphoreType.DMA((7,)), pltpu.SemaphoreType.DMA((4,))],
+        name="gradients",
+    )(*operands)
 
 
 def solution(mesh):

time: 129 us -> 117 us (0.907)
  Pallas kernels: 121 us -> 116 us
  matrix products: 4.04 us -> 0 us
  local copies, waits for them, and re-layouts: 2.48 us -> 0 us
    pallas_call x1, Pallas kernels: 121 us -> 113 us  [body(): pl.pallas_call(functools.partial(kernel, lax.axis_size('tc')), out_shape=...]
    dot_general x4 -> x0, matrix products: 4.04 us -> none  [contract_rows(): lax.dot_general(left, right, (((0,), (0,)), ((), ())), preferred_element_...]
    pallas_call x0 -> x1, Pallas kernels: none -> 3.49 us  [body(): pl.pallas_call(gradients, out_shape=[jax.ShapeDtypeStruct(s, F32) for s i...]
    unnamed x14 -> x0, local copies, waits for them, and re-layouts: 2.48 us -> none
where the time goes in v2:
time: 117 us
  Pallas kernels  116 us (99%)
    pallas_call x1, Pallas kernels, body(): pl.pallas_call(functools.partial(kernel, lax.axis_size('tc')), out_shape=...  113 us
    pallas_call x1, Pallas kernels, body(): pl.pallas_call(gradients, out_shape=[jax.ShapeDtypeStruct(s, F32) for s i...  3.49 us

profile of v2, /device:TPU:8, one launch (start us, length us, event | category | flops | bytes accessed | tf_op | source)
XLA Modules:
  0.0 116.7 jit_solution(7833151512667117338)
XLA Ops:
  0.6 112.6 %chain.1 = (bf16[256,896]{1,0:T(8,128)(2,1)}, bf16[256,256]{1,0:T(8,128)(2,1)}, bf16[256,512]{1,0:T(8,128)(2,1)}, bf16[256,256]{1,0:T(8,128)(2,1)}, bf16[256,896]{1,0:T(8,128)(2,1)}, /*index=5*/bf16[256,896]{1,0:T(8,128)(2,1)}) custom-call(bf16[256,1792]{1,0:T(8,128)(2,1)} %th.1, bf16[256,512]{1,0:T(8,128)(2,1)} %res.1, bf16[1792,512]{1,0:T(8,128)(2,1)} %td.1, ...), custom_call_target="tpu_custom_call" | custom-call | tf_op jit(solution)/shard_map/chain/pallas_call | solution.py:293
  113.2 3.5 %gradients.1 = (f32[256,896]{1,0:T(8,128)}, f32[256,896]{1,0:T(8,128)}, f32[896,256]{1,0:T(8,128)}, f32[256,512]{1,0:T(8,128)}) custom-call(bf16[256,256]{1,0:T(8,128)(2,1)} %x.1, bf16[256,896]{1,0:T(8,128)(2,1)} %get-tuple-element.10.gs, bf16[256,896]{1,0:T(8,128)(2,1)} %get-tuple-element.11.us, bf16[256,896]{1,0:T(8,128)(2,1)} %get-tuple-element.12.hid, ...), custom_call_target="tpu_custom_call" | custom-call | tf_op jit(solution)/shard_map/gradients/pallas_call | solution.py:306

commit v3 on v2

--- a/solution.py
+++ b/solution.py
@@ -13,6 +13,8 @@
 MESH = pl.DeviceIdType.MESH
 N = 16
 OTHERS = N - 1
+FIRST = ((0, 256), (256, 256), (512, 256), (768, 128))
+SECOND = ((0, 384), (384, 384), (768, 128))
 
 
 def dot(a, b):
@@ -34,12 +36,20 @@
     th, res, td, xin, stream, wg, wu, wd, hd,
     o_hid, o_feat, o_sig, o_fg, o_gs, o_us,
     v_th, v_res, v_td, v_x, v_stream, v_wg, v_wu, v_wd, v_hd,
-    f1, p1, r1, g2s, g2, f3, p3, r3, g3s, g3, f4, p4, r4, g5s, g5,
-    f6, p6, r6, g6s, g6, f7, p7, r7, g8s, g8,
+    f3, p3, r3, g3s, g3, f4, p4, r4, g5s, g5, f6, p6, r6, g6s, g6,
     gates, gate_ref, ups, up_ref, by_gate, by_up, s_gate, s_up,
-    load_sem, out_sem, send_sem, recv_sem,
+    load_sem, out_sem, send_sem, recv_sem, *blocks,
 ):
-    tokens = p1.shape[0]
+    first, second = FIRST, SECOND
+    take = lambda n: [blocks.pop(0) for _ in range(n)]
+    blocks = list(blocks)
+    n1, n2 = len(first), len(second)
+    parts1 = list(zip(take(n1), take(n1)))
+    lands1, pairs1, slots1, shares1, g2 = [take(n1) for _ in range(5)]
+    parts7 = list(zip(take(n2), take(n2)))
+    lands7, pairs7, slots7, shares7, g8 = [take(n2) for _ in range(5)]
+
+    tokens = p3.shape[0]
     rows = tokens // N
     fs = wg.shape[1]
     st = lax.axis_index("st")
@@ -78,53 +88,117 @@
 
     lax.fori_loop(1, N, greet, 0)
 
-    def scatter(i, peer, part, slots):
+    zs = N // 2
+    z = lax.rem(st, zs)
+    base = st - z
+    across = {"st": lax.rem(st + zs, N)}
+    half = zs * rows
+    mine = pl.ds(pl.multiple_of(base * rows, half), half)
+    theirs = pl.ds(pl.multiple_of((zs - base) * rows, half), half)
+    owed = []
+
+    def turn(like):
+        owed.append(like)
+        return len(owed) - 1
+
+    def send(i, src, dst, device):
+        pltpu.make_async_remote_copy(
+            src_ref=src, dst_ref=dst,
+            send_sem=send_sem.at[i], recv_sem=recv_sem.at[i],
+            device_id=device, device_id_type=MESH,
+        ).start()
+
+    def each(first, last, fn):
         def one(k, carry):
+            fn(k)
+            return carry
+
+        lax.fori_loop(first, last, one, 0)
+
+    def await_in(i, like):
+        pltpu.make_async_copy(like, like, recv_sem.at[i]).wait()
+
+    def scatter(peer, part, slots):
+        i = turn(slots)
+
+        def one(k):
             p, device = peer(k)
-            pltpu.make_async_remote_copy(
-                src_ref=at_rows(part, p), dst_ref=slots.at[OTHERS - k],
-                send_sem=send_sem.at[i], recv_sem=recv_sem.at[i],
-                device_id=device, device_id_type=MESH,
-            ).start()
-            return carry
-
-        lax.fori_loop(1, N, one, 0)
-
-    def arrived(i, slots):
-        pltpu.make_async_copy(slots, slots, recv_sem.at[i]).wait()
+            send(i, at_rows(part, p), slots.at[OTHERS - k], device)
+
+        each(1, N, one)
+        return i
 
     def summed(i, own, slots):
-        arrived(i, slots)
+        await_in(i, slots)
         total = own
-        for k in range(OTHERS):
+        for k in range(slots.shape[0]):
             total = total + slots[k].astype(F32)
         return total
 
-    def spread(i, peer, share, whole, me):
-        def one(k, carry):
-            device = peer(k)[1]
-            pltpu.make_async_remote_copy(
-                src_ref=share, dst_ref=at_rows(whole, me),
-                send_sem=send_sem.at[i], recv_sem=recv_sem.at[i],
-                device_id=device, device_id_type=MESH,
-            ).start()
-            return carry
-
-        lax.fori_loop(1, N, one, 0)
-
-    def gathered(i, whole):
-        most = whole.at[pl.ds(0, OTHERS * rows), :]
-        pltpu.make_async_copy(most, most, recv_sem.at[i]).wait()
-
-    def sent(i, like):
-        most = like.at[pl.ds(0, OTHERS * rows), :]
-        pltpu.make_async_copy(most, most, send_sem.at[i]).wait()
+    def spread(peer, share, whole, me):
+        i = turn(whole.at[pl.ds(0, OTHERS * rows), :])
+        each(1, N, lambda k: send(i, share, at_rows(whole, me), peer(k)[1]))
+        return i
+
+    def gathered(i):
+        await_in(i, owed[i])
+
+    def swap(part, land):
+        i = turn(land)
+        send(i, part.at[theirs, :], land, across)
+        return i
+
+    def z_peer(k):
+        p = lax.rem(z + k, zs)
+        return p, {"st": base + p}
+
+    def z_scatter(part, slots):
+        i = turn(slots)
+
+        def one(k):
+            p, device = z_peer(k)
+            send(i, at_rows(part, p), slots.at[zs - 1 - k], device)
+
+        each(1, zs, one)
+        return i
+
+    def z_spread(share, whole, me):
+        i = turn(whole.at[pl.ds(0, (zs - 1) * rows), :])
+        each(1, zs, lambda k: send(i, share, at_rows(whole, me), z_peer(k)[1]))
+        return i
+
+    def forward(whole):
+        i = turn(whole.at[pl.ds(0, half), :])
+        send(i, whole.at[mine, :], whole.at[mine, :], across)
+        return i
 
     def put(ref, i, value):
         ref[pl.ds(pl.multiple_of(i * rows, rows), rows), :] = value
 
     def get(ref, i):
         return ref[pl.ds(pl.multiple_of(i * rows, rows), rows), :]
+
+    def reduced(parts, lands, pairs, slots, finish, shares, wholes):
+        turns = [swap(p, land) for (_, p), land in zip(parts, lands)]
+        last = len(parts) - 1
+        for n, (f, _) in enumerate(parts):
+            await_in(turns[n], lands[n])
+            pairs[n][...] = (f[mine, :] + lands[n][...].astype(F32)).astype(BF)
+            turns[n] = z_scatter(pairs[n], slots[n])
+        for n, (f, _) in enumerate(parts):
+            own = get(f, st) + get(lands[n], z).astype(F32)
+            share = finish(n, summed(turns[n], own, slots[n]))
+            shares[n][...] = share
+            if n < last:
+                turns[n] = z_spread(shares[n], wholes[n], st)
+            else:
+                turns[n] = spread(st_peer, shares[n], wholes[n], st)
+            put(wholes[n], st, share)
+        for n in range(last):
+            gathered(turns[n])
+            turns[n] = forward(wholes[n])
+        for i in turns:
+            gathered(i)
 
     outs = []
 
@@ -135,83 +209,87 @@
 
     for c in loads[:3]:
         c.wait()
-    for w, at in ((v_wg, 0), (v_wu, fs)):
-        part = dot(v_x[...], w[...])
-        f1[:, pl.ds(at, fs)] = part
-        p1[:, pl.ds(at, fs)] = part.astype(BF)
-    pl.semaphore_wait(barrier, 2 * OTHERS)
-    scatter(0, st_peer, p1, r1)
+    for (f, p), (at, w) in zip(parts1, first):
+        cols = pl.ds(at, w)
+        part = jnp.concatenate([dot(v_x[...], v_wg[:, cols]), dot(v_x[...], v_wu[:, cols])], axis=1)
+        f[...] = part
+        p[...] = part.astype(BF)
     for c in loads[3:]:
         c.wait()
     f4[...] = dot(v_th[...], v_td[...])
-    both = summed(0, get(f1, st), r1)
-    gate, up = both[:, :fs], both[:, fs:]
-    gates[...] = gate.astype(BF)
-    ups[...] = up.astype(BF)
-    share = (gate * jax.nn.sigmoid(gate) * up).astype(BF)
-    g2s[...] = share
-    spread(1, st_peer, g2s, g2, st)
-    put(g2, st, share)
+    pl.semaphore_wait(barrier, 2 * OTHERS)
+
+    def finish_hidden(n, both):
+        at, w = first[n]
+        gate, up = both[:, :w], both[:, w:]
+        gates[:, pl.ds(at, w)] = gate.astype(BF)
+        ups[:, pl.ds(at, w)] = up.astype(BF)
+        return (gate * jax.nn.sigmoid(gate) * up).astype(BF)
+
+    reduced(parts1, lands1, pairs1, slots1, finish_hidden, shares1, g2)
+    part = 0.0
+    for g, (at, w) in zip(g2, first):
+        part += dot(g[...], v_wd[pl.ds(at, w), :])
+    f3[...] = part
+    p3[...] = part.astype(BF)
+    i = scatter(grp_peer, p3, r3)
     put(gate_ref, st, gates[...])
     put(up_ref, st, ups[...])
-    gathered(1, g2)
-    part = dot(g2[...], v_wd[...])
-    f3[...] = part
-    p3[...] = part.astype(BF)
-    scatter(2, grp_peer, p3, r3)
-    spread(9, st_peer, gates, gate_ref, st)
-    out(g2, o_hid)
-    total = summed(2, get(f3, grp), r3)
+    i_gate = spread(st_peer, gates, gate_ref, st)
+    for g, (at, w) in zip(g2, first):
+        out(g, o_hid.at[:, pl.ds(at, w)])
+    total = summed(i, get(f3, grp), r3)
     share = (v_stream[...].astype(F32) + total).astype(BF)
     g3s[...] = share
-    spread(3, grp_peer, g3s, g3, grp)
+    i = spread(grp_peer, g3s, g3, grp)
     put(g3, grp, share)
-    gathered(3, g3)
+    gathered(i)
     part = dot(g3[...], v_hd[...]) - f4[...]
     f4[...] = part
     p4[...] = part.astype(BF)
-    scatter(4, st_peer, p4, r4)
+    i = scatter(st_peer, p4, r4)
     out(g3, o_feat)
-    total = summed(4, get(f4, st), r4)
+    total = summed(i, get(f4, st), r4)
     share = ((total - v_res[...].astype(F32)) * (1.0 / math.sqrt(tokens))).astype(BF)
     g5s[...] = share
-    spread(5, st_peer, g5s, g5, st)
+    i = spread(st_peer, g5s, g5, st)
     put(g5, st, share)
-    gathered(5, g5)
+    gathered(i)
     part = dot_cols(g5[...], v_hd[...])
     f6[...] = part
     p6[...] = part.astype(BF)
-    scatter(6, grp_peer, p6, r6)
-    spread(10, st_peer, ups, up_ref, st)
+    i = scatter(grp_peer, p6, r6)
+    i_up = spread(st_peer, ups, up_ref, st)
     out(g5, o_sig)
-    share = summed(6, get(f6, grp), r6).astype(BF)
+    share = summed(i, get(f6, grp), r6).astype(BF)
     g6s[...] = share
-    spread(7, grp_peer, g6s, g6, grp)
+    i = spread(grp_peer, g6s, g6, grp)
     put(g6, grp, share)
-    gathered(7, g6)
-    part = dot_cols(g6[...], v_wd[...])
-    f7[...] = part
-    p7[...] = part.astype(BF)
-    scatter(8, st_peer, p7, r7)
+    gathered(i)
+    for (f, p), (at, w) in zip(parts7, second):
+        part = dot_cols(g6[...], v_wd[pl.ds(at, w), :])
+        f[...] = part
+        p[...] = part.astype(BF)
     out(g6, o_fg)
-    gathered(9, gate_ref)
-    gathered(10, up_ref)
-    gate = gate_ref[...].astype(F32)
-    sigma = jax.nn.sigmoid(gate)
-    by_gate[...] = up_ref[...].astype(F32) * (sigma * (1.0 + gate * (1.0 - sigma)))
-    by_up[...] = gate * sigma
-    share = summed(8, get(f7, st), r7).astype(BF)
-    g8s[...] = share
-    spread(11, st_peer, g8s, g8, st)
-    put(g8, st, share)
-    gathered(11, g8)
-    grad = g8[...].astype(F32)
-    s_gate[...] = (grad * by_gate[...]).astype(BF)
-    out(s_gate, o_gs)
-    s_up[...] = (grad * by_up[...]).astype(BF)
-    out(s_up, o_us)
-    for i, like in enumerate((p1, g2, p3, g3, p4, g5, p6, g6, p7, gate_ref, up_ref, g8)):
-        sent(i, like)
+
+    def finish_grad(n, total):
+        if n == 0:
+            gathered(i_gate)
+            gathered(i_up)
+            gate = gate_ref[...].astype(F32)
+            sigma = jax.nn.sigmoid(gate)
+            by_gate[...] = up_ref[...].astype(F32) * (sigma * (1.0 + gate * (1.0 - sigma)))
+            by_up[...] = gate * sigma
+        return total.astype(BF)
+
+    reduced(parts7, lands7, pairs7, slots7, finish_grad, shares7, g8)
+    for made, by, dest in ((s_gate, by_gate, o_gs), (s_up, by_up, o_us)):
+        for g, (at, w) in zip(g8, second):
+            cols = pl.ds(at, w)
+            made[:, cols] = (g[...].astype(F32) * by[:, cols]).astype(BF)
+        out(made, dest)
+    for i, like in enumerate(owed):
+        pltpu.make_async_copy(like, like, send_sem.at[i]).wait()
     for c in outs:
         c.wait()
 
@@ -268,26 +346,37 @@
     def gather_bufs(cols):
         return [vm((rows, cols), BF), vm((tokens, cols), BF)]
 
+    def block_bufs(cuts, of):
+        wide = [w * of for _, w in cuts]
+        return (
+            [vm((tokens, w), F32) for w in wide]
+            + [vm((tokens, w), BF) for w in wide]
+            + [vm((tokens // 2, w), BF) for w in wide]
+            + [vm((tokens // 2, w), BF) for w in wide]
+            + [vm((N // 2 - 1, rows, w), BF) for w in wide]
+            + [vm((rows, w), BF) for _, w in cuts]
+            + [vm((tokens, w), BF) for _, w in cuts]
+        )
+
     staged = [
         vm((rows, a.shape[1]), a.dtype) if i in (1, 4) else vm(a.shape, a.dtype)
         for i, a in enumerate(arguments)
     ]
     scratch = (
         staged
-        + reduce_bufs(2 * fs) + gather_bufs(fs)
         + reduce_bufs(ds) + gather_bufs(ds)
         + reduce_bufs(dt) + gather_bufs(dt)
         + reduce_bufs(ds) + gather_bufs(ds)
-        + reduce_bufs(fs) + gather_bufs(fs)
         + gather_bufs(fs) + gather_bufs(fs)
         + [vm((tokens, fs), F32)] * 2
         + [vm((tokens, fs), BF)] * 2
         + [
             pltpu.SemaphoreType.DMA((9,)),
-            pltpu.SemaphoreType.DMA((6,)),
             pltpu.SemaphoreType.DMA((12,)),
-            pltpu.SemaphoreType.DMA((12,)),
+            pltpu.SemaphoreType.DMA((48,)),
+            pltpu.SemaphoreType.DMA((48,)),
         ]
+        + block_bufs(FIRST, 2) + block_bufs(SECOND, 1)
     )
     shapes = [(tokens, c) for c in (fs, ds, dt, ds, fs, fs)]
     hidden, features, signal, feature_grad, gate_signal, up_signal = pl.pallas_call(

time: 117 us -> 109 us (0.932); the launches traced: 117 us -> 107 us
  Pallas kernels: 116 us -> 107 us
    pallas_call x1, Pallas kernels: 113 us -> 103 us  [body(): pl.pallas_call(functools.partial(kernel, lax.axis_size('tc')), out_shape=...]
where the time goes in v3:
time: 109 us; the launch traced here: 107 us
  Pallas kernels  107 us (98%)
    pallas_call x1, Pallas kernels, body(): pl.pallas_call(functools.partial(kernel, lax.axis_size('tc')), out_shape=...  103 us
    pallas_call x1, Pallas kernels, body(): pl.pallas_call(gradients, out_shape=[jax.ShapeDtypeStruct(s, F32) for s i...  3.49 us

profile of v3, /device:TPU:8, one launch (start us, length us, event | category | flops | bytes accessed | tf_op | source)
XLA Modules:
  0.0 107.4 jit_solution(7764203037925907565)
XLA Ops:
  0.6 103.3 %chain.1 = (bf16[256,896]{1,0:T(8,128)(2,1)}, bf16[256,256]{1,0:T(8,128)(2,1)}, bf16[256,512]{1,0:T(8,128)(2,1)}, bf16[256,256]{1,0:T(8,128)(2,1)}, bf16[256,896]{1,0:T(8,128)(2,1)}, /*index=5*/bf16[256,896]{1,0:T(8,128)(2,1)}) custom-call(bf16[256,1792]{1,0:T(8,128)(2,1)} %th.1, bf16[256,512]{1,0:T(8,128)(2,1)} %res.1, bf16[1792,512]{1,0:T(8,128)(2,1)} %td.1, ...), custom_call_target="tpu_custom_call" | custom-call | tf_op jit(solution)/shard_map/chain/pallas_call | solution.py:382
  103.9 3.5 %gradients.1 = (f32[256,896]{1,0:T(8,128)}, f32[256,896]{1,0:T(8,128)}, f32[896,256]{1,0:T(8,128)}, f32[256,512]{1,0:T(8,128)}) custom-call(bf16[256,256]{1,0:T(8,128)(2,1)} %x.1, bf16[256,896]{1,0:T(8,128)(2,1)} %get-tuple-element.10.gs, bf16[256,896]{1,0:T(8,128)(2,1)} %get-tuple-element.11.us, bf16[256,896]{1,0:T(8,128)(2,1)} %get-tuple-element.12.hid, ...), custom_call_target="tpu_custom_call" | custom-call | tf_op jit(solution)/shard_map/gradients/pallas_call | solution.py:395

commit v4 on v3

--- a/solution.py
+++ b/solution.py
@@ -55,13 +55,30 @@
     st = lax.axis_index("st")
     grp = lax.axis_index("tr") * tc_size + lax.axis_index("tc")
 
+    zs = N // 2
+    z = lax.rem(st, zs)
+    base = st - z
+
+    def from_far(k, length):
+        k = k + 1
+        return length // 2 + (k // 2) * (2 * lax.rem(k, 2) - 1)
+
+    def z_peer(k):
+        p = lax.rem(z + from_far(k, zs), zs)
+        return base + p, {"st": base + p}, p
+
     def st_peer(k):
-        p = lax.rem(st + k, N)
+        p = z_peer(k // 2)[2]
+        p = p + lax.rem(base + zs * (1 - lax.rem(k, 2)), N)
         return p, {"st": p}
 
     def grp_peer(k):
-        p = lax.rem(grp + k, N)
-        return p, {"tr": p // tc_size, "tc": lax.rem(p, tc_size)}
+        trs = N // tc_size
+        tr, tc = lax.axis_index("tr"), lax.axis_index("tc")
+        tr = lax.rem(tr + from_far(lax.rem(k, N // 2) // 2, trs), trs)
+        y, core = tc // 2 + 1 - k // (N // 2), tc + 1 - lax.rem(k, 2)
+        tc = 2 * lax.rem(y, 2) + lax.rem(core, 2)
+        return tr * tc_size + tc, {"tr": tr, "tc": tc}
 
     def at_rows(ref, i):
         return ref.at[pl.ds(pl.multiple_of(i * rows, rows), rows), :]
@@ -86,11 +103,8 @@
             pl.semaphore_signal(barrier, inc=1, device_id=peer(k)[1], device_id_type=MESH)
         return carry
 
-    lax.fori_loop(1, N, greet, 0)
-
-    zs = N // 2
-    z = lax.rem(st, zs)
-    base = st - z
+    lax.fori_loop(0, OTHERS, greet, 0)
+
     across = {"st": lax.rem(st + zs, N)}
     half = zs * rows
     mine = pl.ds(pl.multiple_of(base * rows, half), half)
@@ -108,12 +122,12 @@
             device_id=device, device_id_type=MESH,
         ).start()
 
-    def each(first, last, fn):
+    def each(count, fn):
         def one(k, carry):
             fn(k)
             return carry
 
-        lax.fori_loop(first, last, one, 0)
+        lax.fori_loop(0, count, one, 0)
 
     def await_in(i, like):
         pltpu.make_async_copy(like, like, recv_sem.at[i]).wait()
@@ -123,9 +137,9 @@
 
         def one(k):
             p, device = peer(k)
-            send(i, at_rows(part, p), slots.at[OTHERS - k], device)
-
-        each(1, N, one)
+            send(i, at_rows(part, p), slots.at[k], device)
+
+        each(OTHERS, one)
         return i
 
     def summed(i, own, slots):
@@ -137,7 +151,7 @@
 
     def spread(peer, share, whole, me):
         i = turn(whole.at[pl.ds(0, OTHERS * rows), :])
-        each(1, N, lambda k: send(i, share, at_rows(whole, me), peer(k)[1]))
+        each(OTHERS, lambda k: send(i, share, at_rows(whole, me), peer(k)[1]))
         return i
 
     def gathered(i):
@@ -148,23 +162,19 @@
         send(i, part.at[theirs, :], land, across)
         return i
 
-    def z_peer(k):
-        p = lax.rem(z + k, zs)
-        return p, {"st": base + p}
-
     def z_scatter(part, slots):
         i = turn(slots)
 
         def one(k):
-            p, device = z_peer(k)
-            send(i, at_rows(part, p), slots.at[zs - 1 - k], device)
-
-        each(1, zs, one)
+            _, device, p = z_peer(k)
+            send(i, at_rows(part, p), slots.at[k], device)
+
+        each(zs - 1, one)
         return i
 
     def z_spread(share, whole, me):
         i = turn(whole.at[pl.ds(0, (zs - 1) * rows), :])
-        each(1, zs, lambda k: send(i, share, at_rows(whole, me), z_peer(k)[1]))
+        each(zs - 1, lambda k: send(i, share, at_rows(whole, me), z_peer(k)[1]))
         return i
 
     def forward(whole):

time: 109 us -> 101 us (0.927); the launches traced: 107 us -> 101 us
  Pallas kernels: 107 us -> 100 us
    pallas_call x1, Pallas kernels: 103 us -> 96.9 us  [body(): pl.pallas_call(functools.partial(kernel, lax.axis_size('tc')), out_shape=...]
where the time goes in v4:
time: 101 us
  Pallas kernels  100 us (99%)
    pallas_call x1, Pallas kernels, body(): pl.pallas_call(functools.partial(kernel, lax.axis_size('tc')), out_shape=...  96.9 us
    pallas_call x1, Pallas kernels, body(): pl.pallas_call(gradients, out_shape=[jax.ShapeDtypeStruct(s, F32) for s i...  3.49 us

profile of v4, /device:TPU:8, one launch (start us, length us, event | category | flops | bytes accessed | tf_op | source)
XLA Modules:
  0.0 101.1 jit_solution(15732811335549624329)
XLA Ops:
  0.6 96.9 %chain.1 = (bf16[256,896]{1,0:T(8,128)(2,1)}, bf16[256,256]{1,0:T(8,128)(2,1)}, bf16[256,512]{1,0:T(8,128)(2,1)}, bf16[256,256]{1,0:T(8,128)(2,1)}, bf16[256,896]{1,0:T(8,128)(2,1)}, /*index=5*/bf16[256,896]{1,0:T(8,128)(2,1)}) custom-call(bf16[256,1792]{1,0:T(8,128)(2,1)} %th.1, bf16[256,512]{1,0:T(8,128)(2,1)} %res.1, bf16[1792,512]{1,0:T(8,128)(2,1)} %td.1, ...), custom_call_target="tpu_custom_call" | custom-call | tf_op jit(solution)/shard_map/chain/pallas_call | solution.py:392
  97.6 3.5 %gradients.1 = (f32[256,896]{1,0:T(8,128)}, f32[256,896]{1,0:T(8,128)}, f32[896,256]{1,0:T(8,128)}, f32[256,512]{1,0:T(8,128)}) custom-call(bf16[256,256]{1,0:T(8,128)(2,1)} %x.1, bf16[256,896]{1,0:T(8,128)(2,1)} %get-tuple-element.10.gs, bf16[256,896]{1,0:T(8,128)(2,1)} %get-tuple-element.11.us, bf16[256,896]{1,0:T(8,128)(2,1)} %get-tuple-element.12.hid, ...), custom_call_target="tpu_custom_call" | custom-call | tf_op jit(solution)/shard_map/gradients/pallas_call | solution.py:405

commit v5 on v4

--- a/solution.py
+++ b/solution.py
@@ -14,7 +14,9 @@
 N = 16
 OTHERS = N - 1
 FIRST = ((0, 256), (256, 256), (512, 256), (768, 128))
-SECOND = ((0, 384), (384, 384), (768, 128))
+SECOND = ((0, 256), (256, 256), (512, 256), (768, 128))
+NARROW = ((0, 256),)
+WIDE = ((0, 128), (128, 128), (256, 128), (384, 128))
 
 
 def dot(a, b):
@@ -36,7 +38,7 @@
     th, res, td, xin, stream, wg, wu, wd, hd,
     o_hid, o_feat, o_sig, o_fg, o_gs, o_us,
     v_th, v_res, v_td, v_x, v_stream, v_wg, v_wu, v_wd, v_hd,
-    f3, p3, r3, g3s, g3, f4, p4, r4, g5s, g5, f6, p6, r6, g6s, g6,
+    f3, p3, g3s, g3, f4, p4, g5s, g5, f6, p6, g6s, g6,
     gates, gate_ref, ups, up_ref, by_gate, by_up, s_gate, s_up,
     load_sem, out_sem, send_sem, recv_sem, *blocks,
 ):
@@ -48,6 +50,7 @@
     lands1, pairs1, slots1, shares1, g2 = [take(n1) for _ in range(5)]
     parts7 = list(zip(take(n2), take(n2)))
     lands7, pairs7, slots7, shares7, g8 = [take(n2) for _ in range(5)]
+    r3, r4, r6 = take(len(NARROW)), take(len(WIDE)), take(len(NARROW))
 
     tokens = p3.shape[0]
     rows = tokens // N
@@ -187,6 +190,20 @@
 
     def get(ref, i):
         return ref[pl.ds(pl.multiple_of(i * rows, rows), rows), :]
+
+    def direct(cuts, peer, me, total, part, slots, finish, share, whole, beside, behind):
+        views = [pl.ds(at, w) for at, w in cuts]
+        turns = [scatter(peer, part.at[:, v], b) for v, b in zip(views, slots)]
+        beside()
+        for n, v in enumerate(views):
+            rows_here = pl.ds(pl.multiple_of(me * rows, rows), rows)
+            made = finish(v, summed(turns[n], total[rows_here, v], slots[n]))
+            share[:, v] = made
+            turns[n] = spread(peer, share.at[:, v], whole.at[:, v], me)
+            whole[rows_here, v] = made
+        behind()
+        for i in turns:
+            gathered(i)
 
     def reduced(parts, lands, pairs, slots, finish, shares, wholes):
         turns = [swap(p, land) for (_, p), land in zip(parts, lands)]
@@ -242,40 +259,50 @@
         part += dot(g[...], v_wd[pl.ds(at, w), :])
     f3[...] = part
     p3[...] = part.astype(BF)
-    i = scatter(grp_peer, p3, r3)
-    put(gate_ref, st, gates[...])
-    put(up_ref, st, ups[...])
-    i_gate = spread(st_peer, gates, gate_ref, st)
-    for g, (at, w) in zip(g2, first):
-        out(g, o_hid.at[:, pl.ds(at, w)])
-    total = summed(i, get(f3, grp), r3)
-    share = (v_stream[...].astype(F32) + total).astype(BF)
-    g3s[...] = share
-    i = spread(grp_peer, g3s, g3, grp)
-    put(g3, grp, share)
-    gathered(i)
+    kept = {}
+
+    def start(name, share, whole):
+        put(whole, st, share[...])
+        kept[name] = z_spread(share, whole, st)
+
+    def pass_on(name, whole):
+        gathered(kept[name])
+        kept[name] = forward(whole)
+
+    def beside_down():
+        start("gate", gates, gate_ref)
+        for g, (at, w) in zip(g2, first):
+            out(g, o_hid.at[:, pl.ds(at, w)])
+
+    def finish_features(v, total):
+        return (v_stream[:, v].astype(F32) + total).astype(BF)
+
+    direct(
+        NARROW, grp_peer, grp, f3, p3, r3, finish_features, g3s, g3,
+        beside_down, lambda: start("up", ups, up_ref),
+    )
     part = dot(g3[...], v_hd[...]) - f4[...]
     f4[...] = part
     p4[...] = part.astype(BF)
-    i = scatter(st_peer, p4, r4)
-    out(g3, o_feat)
-    total = summed(i, get(f4, st), r4)
-    share = ((total - v_res[...].astype(F32)) * (1.0 / math.sqrt(tokens))).astype(BF)
-    g5s[...] = share
-    i = spread(st_peer, g5s, g5, st)
-    put(g5, st, share)
-    gathered(i)
+
+    def finish_signal(v, total):
+        return ((total - v_res[:, v].astype(F32)) * (1.0 / math.sqrt(tokens))).astype(BF)
+
+    def beside_error():
+        pass_on("gate", gate_ref)
+        out(g3, o_feat)
+
+    direct(
+        WIDE, st_peer, st, f4, p4, r4, finish_signal, g5s, g5,
+        beside_error, lambda: pass_on("up", up_ref),
+    )
     part = dot_cols(g5[...], v_hd[...])
     f6[...] = part
     p6[...] = part.astype(BF)
-    i = scatter(grp_peer, p6, r6)
-    i_up = spread(st_peer, ups, up_ref, st)
-    out(g5, o_sig)
-    share = summed(i, get(f6, grp), r6).astype(BF)
-    g6s[...] = share
-    i = spread(grp_peer, g6s, g6, grp)
-    put(g6, grp, share)
-    gathered(i)
+    direct(
+        NARROW, grp_peer, grp, f6, p6, r6, lambda v, total: total.astype(BF), g6s, g6,
+        lambda: out(g5, o_sig), lambda: None,
+    )
     for (f, p), (at, w) in zip(parts7, second):
         part = dot_cols(g6[...], v_wd[pl.ds(at, w), :])
         f[...] = part
@@ -284,8 +311,8 @@
 
     def finish_grad(n, total):
         if n == 0:
-            gathered(i_gate)
-            gathered(i_up)
+            gathered(kept["gate"])
+            gathered(kept["up"])
             gate = gate_ref[...].astype(F32)
             sigma = jax.nn.sigmoid(gate)
             by_gate[...] = up_ref[...].astype(F32) * (sigma * (1.0 + gate * (1.0 - sigma)))
@@ -351,7 +378,7 @@
     vm = lambda shape, dtype: pltpu.VMEM(shape, dtype)
 
     def reduce_bufs(cols):
-        return [vm((tokens, cols), F32), vm((tokens, cols), BF), vm((OTHERS, rows, cols), BF)]
+        return [vm((tokens, cols), F32), vm((tokens, cols), BF)]
 
     def gather_bufs(cols):
         return [vm((rows, cols), BF), vm((tokens, cols), BF)]
@@ -387,6 +414,7 @@
             pltpu.SemaphoreType.DMA((48,)),
         ]
         + block_bufs(FIRST, 2) + block_bufs(SECOND, 1)
+        + [vm((OTHERS, rows, w), BF) for _, w in NARROW + WIDE + NARROW]
     )
     shapes = [(tokens, c) for c in (fs, ds, dt, ds, fs, fs)]
     hidden, features, signal, feature_grad, gate_signal, up_signal = pl.pallas_call(

time: 101 us -> 98.5 us (0.975)
  Pallas kernels: 100 us -> 97.7 us
    pallas_call x1, Pallas kernels: 96.9 us -> 94.2 us  [body(): pl.pallas_call(functools.partial(kernel, lax.axis_size('tc')), out_shape=...]
where the time goes in v5:
time: 98.5 us; the launch traced here: 98.4 us
  Pallas kernels  97.7 us (99%)
    pallas_call x1, Pallas kernels, body(): pl.pallas_call(functools.partial(kernel, lax.axis_size('tc')), out_shape=...  94.2 us
    pallas_call x1, Pallas kernels, body(): pl.pallas_call(gradients, out_shape=[jax.ShapeDtypeStruct(s, F32) for s i...  3.49 us

profile of v5, /device:TPU:8, one launch (start us, length us, event | category | flops | bytes accessed | tf_op | source)
XLA Modules:
  0.0 98.4 jit_solution(14681062805729432694)
XLA Ops:
  0.6 94.2 %chain.1 = (bf16[256,896]{1,0:T(8,128)(2,1)}, bf16[256,256]{1,0:T(8,128)(2,1)}, bf16[256,512]{1,0:T(8,128)(2,1)}, bf16[256,256]{1,0:T(8,128)(2,1)}, bf16[256,896]{1,0:T(8,128)(2,1)}, /*index=5*/bf16[256,896]{1,0:T(8,128)(2,1)}) custom-call(bf16[256,1792]{1,0:T(8,128)(2,1)} %th.1, bf16[256,512]{1,0:T(8,128)(2,1)} %res.1, bf16[1792,512]{1,0:T(8,128)(2,1)} %td.1, ...), custom_call_target="tpu_custom_call" | custom-call | tf_op jit(solution)/shard_map/chain/pallas_call | solution.py:420
  94.9 3.5 %gradients.1 = (f32[256,896]{1,0:T(8,128)}, f32[256,896]{1,0:T(8,128)}, f32[896,256]{1,0:T(8,128)}, f32[256,512]{1,0:T(8,128)}) custom-call(bf16[256,256]{1,0:T(8,128)(2,1)} %x.1, bf16[256,896]{1,0:T(8,128)(2,1)} %get-tuple-element.10.gs, bf16[256,896]{1,0:T(8,128)(2,1)} %get-tuple-element.11.us, bf16[256,896]{1,0:T(8,128)(2,1)} %get-tuple-element.12.hid, ...), custom_call_target="tpu_custom_call" | custom-call | tf_op jit(solution)/shard_map/gradients/pallas_call | solution.py:433

commit v6 on v5

--- a/solution.py
+++ b/solution.py
@@ -13,8 +13,8 @@
 MESH = pl.DeviceIdType.MESH
 N = 16
 OTHERS = N - 1
-FIRST = ((0, 256), (256, 256), (512, 256), (768, 128))
-SECOND = ((0, 256), (256, 256), (512, 256), (768, 128))
+FIRST = ((0, 256), (256, 256), (512, 128), (640, 128), (768, 128))
+SECOND = ((0, 384), (384, 256), (640, 128), (768, 128))
 NARROW = ((0, 256),)
 WIDE = ((0, 128), (128, 128), (256, 128), (384, 128))
 
@@ -205,15 +205,24 @@
         for i in turns:
             gathered(i)
 
-    def reduced(parts, lands, pairs, slots, finish, shares, wholes):
-        turns = [swap(p, land) for (_, p), land in zip(parts, lands)]
+    def reduced(parts, lands, pairs, slots, finish, shares, wholes, ready=lambda n: None):
+        turns = [None] + [swap(parts[1][1], lands[1])]
+        turns[0] = scatter(st_peer, parts[0][1], slots[0])
+        turns += [swap(p, land) for (_, p), land in zip(parts[2:], lands[2:])]
         last = len(parts) - 1
-        for n, (f, _) in enumerate(parts):
+        for n, (f, _) in list(enumerate(parts))[1:]:
             await_in(turns[n], lands[n])
             pairs[n][...] = (f[mine, :] + lands[n][...].astype(F32)).astype(BF)
             turns[n] = z_scatter(pairs[n], slots[n])
+        passed = 0
         for n, (f, _) in enumerate(parts):
-            own = get(f, st) + get(lands[n], z).astype(F32)
+            if n == last:
+                gathered(turns[0])
+                turns[0] = forward(wholes[0])
+                passed = 1
+            own = get(f, st)
+            if n:
+                own = own + get(lands[n], z).astype(F32)
             share = finish(n, summed(turns[n], own, slots[n]))
             shares[n][...] = share
             if n < last:
@@ -221,11 +230,12 @@
             else:
                 turns[n] = spread(st_peer, shares[n], wholes[n], st)
             put(wholes[n], st, share)
-        for n in range(last):
+        for n in range(passed, last):
             gathered(turns[n])
             turns[n] = forward(wholes[n])
-        for i in turns:
+        for n, i in enumerate(turns):
             gathered(i)
+            ready(n)
 
     outs = []
 
@@ -319,12 +329,15 @@
             by_up[...] = gate * sigma
         return total.astype(BF)
 
-    reduced(parts7, lands7, pairs7, slots7, finish_grad, shares7, g8)
-    for made, by, dest in ((s_gate, by_gate, o_gs), (s_up, by_up, o_us)):
-        for g, (at, w) in zip(g8, second):
-            cols = pl.ds(at, w)
-            made[:, cols] = (g[...].astype(F32) * by[:, cols]).astype(BF)
-        out(made, dest)
+    def ready_grad(n):
+        at, w = second[n]
+        cols = pl.ds(at, w)
+        grad = g8[n][...].astype(F32)
+        for made, by, dest in ((s_gate, by_gate, o_gs), (s_up, by_up, o_us)):
+            made[:, cols] = (grad * by[:, cols]).astype(BF)
+            out(made.at[:, cols], dest.at[:, cols])
+
+    reduced(parts7, lands7, pairs7, slots7, finish_grad, shares7, g8, ready_grad)
     for i, like in enumerate(owed):
         pltpu.make_async_copy(like, like, send_sem.at[i]).wait()
     for c in outs:
@@ -390,7 +403,7 @@
             + [vm((tokens, w), BF) for w in wide]
             + [vm((tokens // 2, w), BF) for w in wide]
             + [vm((tokens // 2, w), BF) for w in wide]
-            + [vm((N // 2 - 1, rows, w), BF) for w in wide]
+            + [vm((N // 2 - 1 if n else OTHERS, rows, w), BF) for n, w in enumerate(wide)]
             + [vm((rows, w), BF) for _, w in cuts]
             + [vm((tokens, w), BF) for _, w in cuts]
         )
@@ -409,7 +422,7 @@
         + [vm((tokens, fs), BF)] * 2
         + [
             pltpu.SemaphoreType.DMA((9,)),
-            pltpu.SemaphoreType.DMA((12,)),
+            pltpu.SemaphoreType.DMA((16,)),
             pltpu.SemaphoreType.DMA((48,)),
             pltpu.SemaphoreType.DMA((48,)),
         ]

time: 98.5 us -> 95.2 us (0.966)
  Pallas kernels: 97.7 us -> 94.3 us
    pallas_call x1, Pallas kernels: 94.2 us -> 90.9 us  [body(): pl.pallas_call(functools.partial(kernel, lax.axis_size('tc')), out_shape=...]
where the time goes in v6:
time: 95.2 us; the launch traced here: 95 us
  Pallas kernels  94.3 us (99%)
    pallas_call x1, Pallas kernels, body(): pl.pallas_call(functools.partial(kernel, lax.axis_size('tc')), out_shape=...  90.9 us
    pallas_call x1, Pallas kernels, body(): pl.pallas_call(gradients, out_shape=[jax.ShapeDtypeStruct(s, F32) for s i...  3.49 us

profile of v6, /device:TPU:8, one launch (start us, length us, event | category | flops | bytes accessed | tf_op | source)
XLA Modules:
  0.0 95.0 jit_solution(404424789982982615)
XLA Ops:
  0.6 90.9 %chain.1 = (bf16[256,896]{1,0:T(8,128)(2,1)}, bf16[256,256]{1,0:T(8,128)(2,1)}, bf16[256,512]{1,0:T(8,128)(2,1)}, bf16[256,256]{1,0:T(8,128)(2,1)}, bf16[256,896]{1,0:T(8,128)(2,1)}, /*index=5*/bf16[256,896]{1,0:T(8,128)(2,1)}) custom-call(bf16[256,1792]{1,0:T(8,128)(2,1)} %th.1, bf16[256,512]{1,0:T(8,128)(2,1)} %res.1, bf16[1792,512]{1,0:T(8,128)(2,1)} %td.1, ...), custom_call_target="tpu_custom_call" | custom-call | tf_op jit(solution)/shard_map/chain/pallas_call | solution.py:433
  91.5 3.5 %gradients.1 = (f32[256,896]{1,0:T(8,128)}, f32[256,896]{1,0:T(8,128)}, f32[896,256]{1,0:T(8,128)}, f32[256,512]{1,0:T(8,128)}) custom-call(bf16[256,256]{1,0:T(8,128)(2,1)} %x.1, bf16[256,896]{1,0:T(8,128)(2,1)} %get-tuple-element.10.gs, bf16[256,896]{1,0:T(8,128)(2,1)} %get-tuple-element.11.us, bf16[256,896]{1,0:T(8,128)(2,1)} %get-tuple-element.12.hid, ...), custom_call_target="tpu_custom_call" | custom-call | tf_op jit(solution)/shard_map/gradients/pallas_call | solution.py:446

commit v7 on v6

--- a/solution.py
+++ b/solution.py
@@ -13,8 +13,8 @@
 MESH = pl.DeviceIdType.MESH
 N = 16
 OTHERS = N - 1
-FIRST = ((0, 256), (256, 256), (512, 128), (640, 128), (768, 128))
-SECOND = ((0, 384), (384, 256), (640, 128), (768, 128))
+FIRST = ((0, 256), (256, 128), (384, 128), (512, 128), (640, 128), (768, 128))
+SECOND = ((0, 384), (384, 128), (512, 128), (640, 128), (768, 128))
 NARROW = ((0, 256),)
 WIDE = ((0, 128), (128, 128), (256, 128), (384, 128))
 
@@ -422,9 +422,9 @@
         + [vm((tokens, fs), BF)] * 2
         + [
             pltpu.SemaphoreType.DMA((9,)),
-            pltpu.SemaphoreType.DMA((16,)),
-            pltpu.SemaphoreType.DMA((48,)),
-            pltpu.SemaphoreType.DMA((48,)),
+            pltpu.SemaphoreType.DMA((24,)),
+            pltpu.SemaphoreType.DMA((64,)),
+            pltpu.SemaphoreType.DMA((64,)),
         ]
         + block_bufs(FIRST, 2) + block_bufs(SECOND, 1)
         + [vm((OTHERS, rows, w), BF) for _, w in NARROW + WIDE + NARROW]

time: 95.2 us -> 95.5 us (level)
  no operation moved by 1% of the time
where the time goes in v7:
time: 95.5 us; the launch traced here: 95.4 us
  Pallas kernels  94.7 us (99%)
    pallas_call x1, Pallas kernels, body(): pl.pallas_call(functools.partial(kernel, lax.axis_size('tc')), out_shape=...  91.2 us
    pallas_call x1, Pallas kernels, body(): pl.pallas_call(gradients, out_shape=[jax.ShapeDtypeStruct(s, F32) for s i...  3.49 us

profile of v7, /device:TPU:8, one launch (start us, length us, event | category | flops | bytes accessed | tf_op | source)
XLA Modules:
  0.0 95.4 jit_solution(10168570235072392689)
XLA Ops:
  0.6 91.2 %chain.1 = (bf16[256,896]{1,0:T(8,128)(2,1)}, bf16[256,256]{1,0:T(8,128)(2,1)}, bf16[256,512]{1,0:T(8,128)(2,1)}, bf16[256,256]{1,0:T(8,128)(2,1)}, bf16[256,896]{1,0:T(8,128)(2,1)}, /*index=5*/bf16[256,896]{1,0:T(8,128)(2,1)}) custom-call(bf16[256,1792]{1,0:T(8,128)(2,1)} %th.1, bf16[256,512]{1,0:T(8,128)(2,1)} %res.1, bf16[1792,512]{1,0:T(8,128)(2,1)} %td.1, ...), custom_call_target="tpu_custom_call" | custom-call | tf_op jit(solution)/shard_map/chain/pallas_call | solution.py:433
  91.9 3.5 %gradients.1 = (f32[256,896]{1,0:T(8,128)}, f32[256,896]{1,0:T(8,128)}, f32[896,256]{1,0:T(8,128)}, f32[256,512]{1,0:T(8,128)}) custom-call(bf16[256,256]{1,0:T(8,128)(2,1)} %x.1, bf16[256,896]{1,0:T(8,128)(2,1)} %get-tuple-element.10.gs, bf16[256,896]{1,0:T(8,128)(2,1)} %get-tuple-element.11.us, bf16[256,896]{1,0:T(8,128)(2,1)} %get-tuple-element.12.hid, ...), custom_call_target="tpu_custom_call" | custom-call | tf_op jit(solution)/shard_map/gradients/pallas_call | solution.py:446
